TPU v7x, 32 devices: a whole 2x2x4 slice. The times are simulated.
32 devices in a mesh: seg: 16 (over z, x, core), freq: 2 (over y).
Axes of the slice: x: 2, y: 2, z: 4, core: 2. Of those that a mesh axis runs over, the one named last changes fastest.
Arguments:
- coarse: float32 [64, 128, 2048], P('seg', None, 'freq'), may hold values from 0.5 to 8
- offsets: int32 [64, 32], replicated, may hold values from -8 to 8, as said below
Outputs:
- fine: float32 [32, 128, 2048], P(None, 'seg', 'freq')
- peaks: float32 [128], P('seg')
Inputs may be any that keep to these rules, and one draw needn't show every extreme that they name: `offsets`: every entry lies in -8 to 8, and both ends occur in every draw.
All inputs are finite; a program needn't handle non-finite values.
Results may differ from a plain program's by a relative error of at most 0.0003.
Values sent between devices are 32-bit elements; how exact they have to be, the bound alone decides.
A program may use at most 128 MiB of HBM per device.

v0:
```python
import functools

import jax
import jax.numpy as jnp
from jax import lax
from jax.experimental import pallas as pl
from jax.experimental.pallas import tpu as pltpu
from jax.sharding import PartitionSpec as P

HALO = 8
EDGE = 128
SHIFTS = 2 * HALO + 1
PLANES = 4
PAIR = 2
ORDER = (
    ("part", 0, 0),
    ("part", 0, 1),
    ("part", 1, 0),
    ("part", 2, 0),
    ("part", 1, 1),
    ("part", 2, 1),
    ("tail", 1, 0),
    ("tail", 2, 1),
    ("tail", 1, 1),
)
TAILS = (1, 2)
PASSED = 5
CHUNK = EDGE // 2
MESH = pl.DeviceIdType.MESH


def partner(me, step, count):
    result = me
    bit = 1
    while bit < count:
        wanted = (step // bit) % 2 if isinstance(step, int) else lax.rem(step // bit, 2)
        held = lax.rem(me // bit, 2)
        result = result + bit * wanted * (1 - 2 * held)
        bit *= 2
    return result


def kernel(
    nseg,
    nfreq,
    parts,
    coarse,
    offsets,
    total,
    maps,
    low,
    high,
    shifted,
    turned,
    chunks,
    passed,
    tops,
    shifts,
    own_sem,
    shifts_sem,
    send_sem,
    edge_recv,
    pair_recv,
    part_recv,
    tail_recv,
    halo_send,
    halo_recv,
    top_send,
    top_recv,
    near_sem,
    far_sem,
    band_sem,
    pass_send,
    pass_recv,
):
    local_segs = coarse.shape[0]
    spins = total.shape[0] - 1
    rows, bins = total.shape[1:]
    scale = 1.0 / (nseg * local_segs)
    size = nseg // PLANES
    begins = [sum(parts[:place]) for place in range(len(parts))]
    me = lax.axis_index("seg")
    core = lax.rem(me, PAIR)
    band = lax.axis_index("freq")
    plane = me // size
    inner = lax.rem((plane + 1) // 2, 2) == 1
    outer = jnp.logical_not(inner)
    last_group = jnp.where(inner, 3, 2)
    last = (last_group + 1) * size - PAIR

    early = EDGE if nfreq <= 2 else bins
    width = bins - early
    edge_at = jnp.where(band == 0, bins - early, 0)
    rest_at = jnp.where(band == 0, 0, early)

    def each(begin, end, act):
        @pl.loop(begin, end)
        def _(step):
            act(step)

    def greet(step, sem):
        pl.semaphore_signal(
            sem, inc=1, device_id={"seg": partner(me, step, nseg), "freq": band}, device_id_type=MESH
        )

    def greet_bands(sem):
        for step in range(1, nfreq):
            pl.semaphore_signal(
                sem, inc=1, device_id={"seg": me, "freq": lax.rem(band + step, nfreq)}, device_id_type=MESH
            )

    def send(step, begin, count, first, segs, received):
        other = partner(me, step, nseg)
        columns = pl.ds(pl.multiple_of(begin, EDGE), count)
        rows_of = pl.ds(pl.multiple_of(other * rows, rows), rows)
        members = pl.ds(first, segs)
        pltpu.make_async_remote_copy(
            src_ref=coarse.at[members, rows_of, columns],
            dst_ref=maps.at[step, members, :, columns],
            send_sem=send_sem,
            recv_sem=received,
            device_id={"seg": other, "freq": band},
            device_id_type=MESH,
        ).start()

    def send_edge(step):
        send(step, edge_at, early, 0, local_segs, edge_recv.at[step // size])

    def send_rest(step):
        if width:
            send(step, rest_at, width, 0, local_segs, pair_recv.at[step // PAIR])

    def part_sem(pair, place):
        return part_recv.at[place - 1] if place else pair_recv.at[pair]

    def send_lead(group):
        pair = group * size // PAIR
        if width:
            for target, kept in enumerate(TAILS):
                send(step_to(pair, target), rest_at, width, 0, local_segs - kept, pair_recv.at[pair])

    def send_lead_passing(mine):
        pair = 3 * size // PAIR
        step = pair * PAIR
        send(step, rest_at, width - passed_columns, 0, 1, pair_recv.at[pair])
        send(step, rest_at, width, 1, local_segs - TAILS[mine] - 1, pair_recv.at[pair])
        send(step + 1, rest_at, width, 0, local_segs - TAILS[1 - mine], pair_recv.at[pair])

    def step_to(pair, target):
        return pair * PAIR + lax.rem(core + target, PAIR)

    def send_ends(group):
        pair = (group + 1) * size // PAIR - 1

        def part(place, target):
            send(step_to(pair, target), rest_at, width, begins[place], parts[place], part_sem(pair, place))

        def tail(left, target):
            step = step_to(group * size // PAIR, target)
            send(step, rest_at, width, local_segs - left, 1, tail_recv.at[left - 1])

        if width:
            for act, *args in ORDER:
                (part if act == "part" else tail)(*args)

    passes = nfreq == 2
    passed_columns = passed.shape[2]
    passed_at = bins - passed_columns

    def pass_on(source, target, ref, sent, received):
        other = partner(me, 3 * size, nseg)
        return pltpu.make_async_remote_copy(
            src_ref=source,
            dst_ref=ref,
            send_sem=sent,
            recv_sem=received,
            device_id={"seg": me if target == 0 else other, "freq": target},
            device_id_type=MESH,
        )

    def pass_first():
        rows_of = pl.ds(pl.multiple_of(partner(me, 3 * size, nseg) * rows, rows), rows)
        source = coarse.at[pl.ds(0, 1), rows_of, pl.ds(passed_at, passed_columns)]
        return pass_on(source, 0, passed, send_sem, pass_recv)

    def pass_second():
        there = maps.at[3 * size, pl.ds(0, 1), :, pl.ds(passed_at, passed_columns)]
        return pass_on(passed, 1, there, pass_send, pair_recv.at[3 * size // PAIR])

    def wait_for(there, sem):
        pltpu.make_async_copy(there, there, sem).wait()

    def wait_edges(group, first):
        wait_for(maps.at[pl.ds(group * size + first, size - first), :, :, pl.ds(0, early)], edge_recv.at[group])

    def wait_rest(step, steps, segs, sem):
        if width:
            wait_for(maps.at[pl.ds(step, steps), pl.ds(0, segs), :, pl.ds(0, width)], sem)

    def upward(group):
        members = pl.ds(group * size, size)
        return pltpu.make_async_remote_copy(
            src_ref=maps.at[members, :, :, pl.ds(bins - EDGE, EDGE)],
            dst_ref=low.at[members],
            send_sem=halo_send.at[0],
            recv_sem=halo_recv.at[0, group],
            device_id={"seg": me, "freq": band + 1},
            device_id_type=MESH,
        )

    def downward(group):
        members = pl.ds(group * size, size)
        way = halo_send.shape[0] - 1
        return pltpu.make_async_remote_copy(
            src_ref=maps.at[members, :, :, pl.ds(0, EDGE)],
            dst_ref=high.at[members],
            send_sem=halo_send.at[way],
            recv_sem=halo_recv.at[way, group],
            device_id={"seg": me, "freq": band - 1},
            device_id_type=MESH,
        )

    def forward(group):
        @pl.when(band < nfreq - 1)
        def _():
            upward(group).start()

        @pl.when(band > 0)
        def _():
            downward(group).start()

    def wait_halo(group):
        @pl.when(band < nfreq - 1)
        def _():
            downward(group).wait_recv()

        @pl.when(band > 0)
        def _():
            upward(group).wait_recv()

    barrier = pltpu.get_barrier_semaphore()

    @pl.when(inner)
    def _():
        for step in range(3 * size, 3 * size + PAIR):
            greet(step, barrier)
        for step in range(size, 2 * size):
            greet(step, barrier)
        pl.semaphore_wait(barrier, PAIR)
        for step in range(3 * size, 3 * size + PAIR):
            send_edge(step)
        if passes:
            for mine in range(PAIR):

                @pl.when(jnp.logical_and(band == 1, core == mine))
                def _():
                    send_lead_passing(mine)

            @pl.when(band == 0)
            def _():
                send_lead(3)

        else:
            send_lead(3)

    @pl.when(outer)
    def _():
        greet_bands(barrier)
        pl.semaphore_wait(barrier, size + nfreq - 1)
        each(size, 2 * size, lambda step: greet(step, near_sem))
        greet_bands(band_sem)
        each(size, 2 * size, send_edge)
        each(size, size + PAIR, send_rest)

    own = pltpu.make_async_copy(
        coarse.at[:, pl.ds(pl.multiple_of(me * rows, rows), rows), :], maps.at[0], own_sem
    )
    own.start()
    load_shifts = pltpu.make_async_copy(offsets, shifts, shifts_sem)
    load_shifts.start()
    total[...] = jnp.zeros_like(total)

    @pl.when(band == 0)
    def _():
        low[...] = jnp.zeros_like(low)

    @pl.when(band == nfreq - 1)
    def _():
        high[...] = jnp.zeros_like(high)

    @pl.when(inner)
    def _():
        pl.semaphore_wait(near_sem, size)
        greet(3 * size, far_sem)
        pl.semaphore_wait(far_sem, 1)
        greet(size, near_sem)
        each(3 * size + PAIR, nseg, send_edge)
        each(2 * size, 3 * size, send_edge)
        each(size, 2 * size, send_edge)
        each(1, size, send_edge)
        each(1, 2 * size, send_rest)
        send_lead(2)
        if nfreq > 1:
            pl.semaphore_wait(band_sem, 1)
        if passes:

            @pl.when(band == 1)
            def _():
                pass_first().start()

            @pl.when(band == 0)
            def _():
                pass_first().wait_recv()
                pass_second().start()

        each(2 * size + PAIR, 3 * size - PAIR, send_rest)
        send_ends(2)
        each(3 * size + PAIR, 4 * size - PAIR, send_rest)
        send_ends(3)

    @pl.when(outer)
    def _():
        if nfreq > 1:
            pl.semaphore_wait(band_sem, nfreq - 1)
            greet(size, band_sem)
        pl.semaphore_wait(near_sem, 1)
        each(2 * size, nseg, send_edge)
        each(1, size, send_edge)
        each(1, size, send_rest)
        each(size + PAIR, nseg, send_rest)

    lane = lax.broadcasted_iota(jnp.int32, (rows, EDGE), 1)

    def column_of(step, seg):
        return partner(me, step, nseg) * local_segs + seg

    def ring_of(step, seg):
        return jnp.where(lane < EDGE // 2, high[step, seg], low[step, seg])

    def add(lines):
        columns = [column_of(step, seg) for step, seg in lines]
        for slot, (step, seg) in enumerate(lines):
            line = jnp.concatenate([maps[step, seg], ring_of(step, seg)], axis=1)
            for shift in range(-HALO, HALO + 1):
                turned_line = line if shift == 0 else pltpu.roll(line, (-shift) % (bins + EDGE), 1)
                shifted[slot, HALO + shift] = turned_line[:, :bins]

        @pl.loop(0, spins, unroll=4)
        def _(spin):
            value = total[spin]
            for slot, column in enumerate(columns):
                value = value + shifted[slot, HALO + shifts[spin, column]]
            total[spin] = value

    tiles = bins // EDGE
    first_half = lane < CHUNK

    def turn_totals():
        @pl.loop(0, spins // 2, unroll=8)
        def _(pair):
            blocks = []
            for at in range(0, bins, EDGE):
                one = total[2 * pair, :, at : at + EDGE]
                two = total[2 * pair + 1, :, at : at + EDGE]
                blocks.append(jnp.where(first_half, one, pltpu.roll(two, CHUNK, 1)))
                blocks.append(jnp.where(first_half, pltpu.roll(one, CHUNK, 1), two))
            square = jnp.concatenate(blocks, axis=0).T
            turned[2 * pair] = square[:CHUNK]
            turned[2 * pair + 1] = square[CHUNK:]

    def turn_back():
        @pl.loop(0, spins // 2, unroll=8)
        def _(pair):
            square = jnp.concatenate([turned[2 * pair], turned[2 * pair + 1]], axis=0).T
            for tile in range(tiles):
                at = tile * EDGE
                even = square[2 * tile * rows : (2 * tile + 1) * rows]
                odd = square[(2 * tile + 1) * rows : (2 * tile + 2) * rows]
                total[2 * pair, :, at : at + EDGE] = jnp.where(first_half, even, pltpu.roll(odd, CHUNK, 1))
                total[2 * pair + 1, :, at : at + EDGE] = jnp.where(first_half, pltpu.roll(even, CHUNK, 1), odd)

    def add_turned(lines, best=None):
        columns = [column_of(step, seg) for step, seg in lines]
        own_half = lane < CHUNK + CHUNK // 2
        next_part = jnp.logical_and(lane >= CHUNK, own_half)
        for slot, (step, seg) in enumerate(lines):
            whole = [maps[step, seg, :, at : at + EDGE] for at in range(0, bins, EDGE)] + [ring_of(step, seg)]
            half = [pltpu.roll(tile, CHUNK, 1) for tile in whole]
            blocks = []
            for tile in range(tiles):
                blocks.append(jnp.where(own_half, whole[tile], whole[tile - 1]))
                blocks.append(jnp.where(next_part, half[tile + 1], half[tile]))
            square = jnp.concatenate(blocks, axis=0).T
            chunks[slot, :HALO] = square[EDGE - HALO :]
            chunks[slot, HALO:] = square[: CHUNK + HALO]

        def spindown(spin, best):
            value = turned[spin]
            for slot, column in enumerate(columns):
                value = value + chunks[slot, pl.ds(HALO + shifts[spin, column], CHUNK)]
            if best is not None:
                value = value * scale
                best = jnp.maximum(best, value)
            turned[spin] = value
            return best

        return lax.fori_loop(0, spins, spindown, best, unroll=8)

    wait_edges(1, 0)
    forward(1)
    own.wait()
    wait_edges(0, 1)
    forward(0)
    wait_edges(3, 0)
    forward(3)
    wait_edges(2, 0)
    forward(2)
    load_shifts.wait()

    pairs = size // PAIR
    opens = 3 * pairs - 1
    wait_halo(0)
    wait_rest(1, PAIR - 1, local_segs, pair_recv.at[0])

    @pl.loop(0, 4 * pairs - 1)
    def _(turn):
        group = jnp.where(turn < 2 * pairs, turn // pairs, jnp.where(turn < opens, last_group, 5 - last_group))
        member = jnp.where(turn < opens, lax.rem(turn, pairs), turn - opens)
        pair = group * pairs + member

        @pl.when(jnp.logical_and(turn > 0, member == 0))
        def _():
            wait_halo(group)

        def take(segs, waits):
            @pl.when(waits)
            def _():
                wait_rest(PAIR, PAIR, segs, pair_recv.at[pair])

            @pl.loop(0, PAIR)
            def _(core):
                add([(pair * PAIR + core, seg) for seg in range(segs)])

        @pl.when(turn != 2 * pairs)
        def _():
            take(local_segs, turn > 0)

        for target, kept in enumerate(TAILS):

            @pl.when(jnp.logical_and(turn == 2 * pairs, core == target))
            def _():
                take(local_segs - kept, True)

    def lines_of(place):
        return [(last + source, begins[place] + seg) for source in range(PAIR) for seg in range(parts[place])]

    turn_totals()
    def tails(left):
        wait_rest(PAIR, PAIR, 1, tail_recv.at[left - 1])
        return [(last_group * size + source, local_segs - left) for source in range(PAIR)]

    for place, segs in enumerate(parts):
        wait_rest(PAIR, PAIR, segs, part_sem(last // PAIR, place))
        add_turned(lines_of(place))

    @pl.when(core == PAIR - 1)
    def _():
        for left in range(TAILS[-1], 1, -1):
            add_turned(tails(left))

    best = add_turned(tails(1), jnp.full((CHUNK, EDGE), -jnp.inf, jnp.float32))
    top = best[:rows]
    for begin in range(rows, CHUNK, rows):
        top = jnp.maximum(top, best[begin : begin + rows])
    tops[0] = top

    def tell(step):
        return pltpu.make_async_remote_copy(
            src_ref=tops.at[0],
            dst_ref=tops.at[step],
            send_sem=top_send.at[step - 1],
            recv_sem=top_recv.at[step - 1],
            device_id={"seg": me, "freq": lax.rem(band + step, nfreq)},
            device_id_type=MESH,
        )

    for step in range(1, nfreq):
        tell(step).start()

    turn_back()
    sent = coarse.at[:, pl.ds(0, (nseg - 1) * rows), :]
    wait_for(sent, send_sem)

    @pl.when(band < nfreq - 1)
    def _():
        wait_for(low, halo_send.at[0])

    @pl.when(band > 0)
    def _():
        wait_for(high, halo_send.at[halo_send.shape[0] - 1])

    if passes:

        @pl.when(jnp.logical_and(inner, band == 0))
        def _():
            pass_second().wait_send()

    for step in range(1, nfreq):
        tell(step).wait()
    top = tops[0]
    for step in range(1, nfreq):
        top = jnp.maximum(top, tops[step])
    total[spins, :, :EDGE] = top


def finish(total, fine, peaks, line, sem, line_sem):
    spins, rows = fine.shape[:2]
    write = pltpu.make_async_copy(total.at[pl.ds(0, spins)], fine, sem)
    write.start()
    top = jnp.max(total[spins, :, :EDGE], axis=0, keepdims=True)
    apart = EDGE // 2
    while apart >= rows:
        top = jnp.maximum(top, pltpu.roll(top, apart, 1))
        apart //= 2
    line[...] = top[0, :rows]
    write_line = pltpu.make_async_copy(line, peaks, line_sem)
    write_line.start()
    write.wait()
    write_line.wait()


def solution(mesh):
    nseg, nfreq = mesh.shape["seg"], mesh.shape["freq"]

    def on_device(coarse, offsets):
        local_segs, points, bins = coarse.shape
        rows = points // nseg
        spins = offsets.shape[1]
        parts = (local_segs - 2, 1, 1)
        ways = 1 if nfreq <= 2 else 2
        if rows * bins != EDGE * CHUNK or nseg % (2 * PAIR * PLANES) or spins % 2:
            raise ValueError("unsupported shape")
        hbm = pl.BlockSpec(memory_space=pltpu.HBM)
        vmem = pl.BlockSpec(memory_space=pltpu.VMEM)
        dma = pltpu.SemaphoreType.DMA
        signal = pltpu.SemaphoreType.REGULAR
        total = pl.pallas_call(
            functools.partial(kernel, nseg, nfreq, parts),
            out_shape=jax.ShapeDtypeStruct((spins + 1, rows, bins), jnp.float32),
            in_specs=[hbm, hbm],
            out_specs=vmem,
            scratch_shapes=[
                pltpu.VMEM((nseg, local_segs, rows, bins), jnp.float32),
                pltpu.VMEM((nseg, local_segs, rows, EDGE), jnp.float32),
                pltpu.VMEM((nseg, local_segs, rows, EDGE), jnp.float32),
                pltpu.VMEM((local_segs, SHIFTS, rows, bins), jnp.float32),
                pltpu.VMEM((spins, CHUNK, EDGE), jnp.float32),
                pltpu.VMEM((PAIR * max(parts), CHUNK + 2 * HALO, EDGE), jnp.float32),
                pltpu.VMEM((1, rows, bins * PASSED // 8), jnp.float32),
                pltpu.VMEM((nfreq, rows, EDGE), jnp.float32),
                pltpu.SMEM(offsets.shape[::-1], jnp.int32),
                dma,
                dma,
                dma,
                dma((PLANES,)),
                dma((nseg // PAIR,)),
                dma((len(parts) - 1,)),
                dma((max(TAILS),)),
                dma((ways,)),
                dma((ways, PLANES)),
                dma((max(nfreq - 1, 1),)),
                dma((max(nfreq - 1, 1),)),
                signal,
                signal,
                signal,
                dma,
                dma,
            ],
            compiler_params=pltpu.CompilerParams(
                collective_id=0, has_side_effects=True, vmem_limit_bytes=32 << 20
            ),
        )(pltpu.with_memory_space_constraint(coarse, pltpu.HBM), pltpu.with_memory_space_constraint(offsets.T, pltpu.HBM))
        return pl.pallas_call(
            finish,
            out_shape=(
                jax.ShapeDtypeStruct((spins, rows, bins), jnp.float32),
                jax.ShapeDtypeStruct((rows,), jnp.float32),
            ),
            in_specs=[vmem],
            out_specs=(hbm, hbm),
            scratch_shapes=[pltpu.VMEM((rows,), jnp.float32), dma, dma],
            compiler_params=pltpu.CompilerParams(vmem_limit_bytes=8 << 20),
        )(total)

    return jax.shard_map(
        on_device,
        mesh=mesh,
        in_specs=(P("seg", None, "freq"), P()),
        out_specs=(P(None, "seg", "freq"), P("seg")),
        check_vma=False,
    )
```

profile of v0, /device:TPU:8, one launch (start us, length us, event | category | flops | bytes accessed | tf_op | source)
XLA Modules:
  0.0 52.6 jit_solution(16774337605892444997)
XLA Ops:
  0.6 50.9 %shard_map.41.total = f32[33,8,1024]{2,1,0:T(8,128)S(1)} custom-call(f32[4,128,1024]{2,1,0:T(8,128)} %coarse.1, s32[32,64]{1,0:T(8,128)} %bitcast.1), custom_call_target="tpu_custom_call" | custom-call | tf_op jit(solution)/shard_map/pallas_call | solution.py:547
  51.6 1.0 %shard_map.42 = (f32[32,8,1024]{2,1,0:T(8,128)}, f32[8]{0:T(128)}) custom-call(f32[33,8,1024]{2,1,0:T(8,128)S(1)} %shard_map.41.total), custom_call_target="tpu_custom_call" | custom-call | tf_op jit(solution)/shard_map/pallas_call | solution.py:583
where the time goes:
time: 53 us; the launch traced here: 52.6 us
  Pallas kernels  51.9 us (98%)
  between operations  0.64 us (1%)
    pallas_call x1, Pallas kernels, on_device(): pl.pallas_call(functools.partial(kernel, nseg, nfreq, parts), out_shape=j...  50.9 us

commit v1 on v0

--- a/solution.py
+++ b/solution.py
@@ -461,12 +461,17 @@
 
     for place, segs in enumerate(parts):
         wait_rest(PAIR, PAIR, segs, part_sem(last // PAIR, place))
-        add_turned(lines_of(place))
-
-    @pl.when(core == PAIR - 1)
-    def _():
-        for left in range(TAILS[-1], 1, -1):
-            add_turned(tails(left))
+        if place < len(parts) - 1:
+            add_turned(lines_of(place))
+
+    for target, kept in enumerate(TAILS):
+
+        @pl.when(core == target)
+        def _():
+            lines = lines_of(len(parts) - 1)
+            for left in range(kept, 1, -1):
+                lines = lines + tails(left)
+            add_turned(lines)
 
     best = add_turned(tails(1), jnp.full((CHUNK, EDGE), -jnp.inf, jnp.float32))
     top = best[:rows]

time: 53 us -> 53 us (level)
  no operation moved by 1% of the time
where the time goes in v1:
time: 53 us; the launch traced here: 52.6 us
  Pallas kernels  51.9 us (98%)
  between operations  0.64 us (1%)
    pallas_call x1, Pallas kernels, on_device(): pl.pallas_call(functools.partial(kernel, nseg, nfreq, parts), out_shape=j...  50.9 us

profile of v1, /device:TPU:8, one launch (start us, length us, event | category | flops | bytes accessed | tf_op | source)
XLA Modules:
  0.0 52.6 jit_solution(14872776519688118601)
XLA Ops:
  0.6 50.9 %shard_map.41.total = f32[33,8,1024]{2,1,0:T(8,128)S(1)} custom-call(f32[4,128,1024]{2,1,0:T(8,128)} %coarse.1, s32[32,64]{1,0:T(8,128)} %bitcast.1), custom_call_target="tpu_custom_call" | custom-call | tf_op jit(solution)/shard_map/pallas_call | solution.py:552
  51.6 1.0 %shard_map.42 = (f32[32,8,1024]{2,1,0:T(8,128)}, f32[8]{0:T(128)}) custom-call(f32[33,8,1024]{2,1,0:T(8,128)S(1)} %shard_map.41.total), custom_call_target="tpu_custom_call" | custom-call | tf_op jit(solution)/shard_map/pallas_call | solution.py:588

commit v2 on v1

--- a/solution.py
+++ b/solution.py
@@ -54,6 +54,7 @@
     turned,
     chunks,
     passed,
+    ahead,
     tops,
     shifts,
     own_sem,
@@ -72,6 +73,7 @@
     band_sem,
     pass_send,
     pass_recv,
+    ahead_sem,
 ):
     local_segs = coarse.shape[0]
     spins = total.shape[0] - 1
@@ -109,13 +111,13 @@
                 sem, inc=1, device_id={"seg": me, "freq": lax.rem(band + step, nfreq)}, device_id_type=MESH
             )
 
-    def send(step, begin, count, first, segs, received):
+    def send(step, begin, count, first, segs, received, held=None):
         other = partner(me, step, nseg)
         columns = pl.ds(pl.multiple_of(begin, EDGE), count)
         rows_of = pl.ds(pl.multiple_of(other * rows, rows), rows)
         members = pl.ds(first, segs)
         pltpu.make_async_remote_copy(
-            src_ref=coarse.at[members, rows_of, columns],
+            src_ref=coarse.at[members, rows_of, columns] if held is None else held.at[step - 3 * size, members, :, columns],
             dst_ref=maps.at[step, members, :, columns],
             send_sem=send_sem,
             recv_sem=received,
@@ -123,8 +125,8 @@
             device_id_type=MESH,
         ).start()
 
-    def send_edge(step):
-        send(step, edge_at, early, 0, local_segs, edge_recv.at[step // size])
+    def send_edge(step, held=None):
+        send(step, edge_at, early, 0, local_segs, edge_recv.at[step // size], held)
 
     def send_rest(step):
         if width:
@@ -133,18 +135,18 @@
     def part_sem(pair, place):
         return part_recv.at[place - 1] if place else pair_recv.at[pair]
 
-    def send_lead(group):
+    def send_lead(group, held=None):
         pair = group * size // PAIR
         if width:
             for target, kept in enumerate(TAILS):
-                send(step_to(pair, target), rest_at, width, 0, local_segs - kept, pair_recv.at[pair])
-
-    def send_lead_passing(mine):
+                send(step_to(pair, target), rest_at, width, 0, local_segs - kept, pair_recv.at[pair], held)
+
+    def send_lead_passing(mine, held):
         pair = 3 * size // PAIR
         step = pair * PAIR
-        send(step, rest_at, width - passed_columns, 0, 1, pair_recv.at[pair])
-        send(step, rest_at, width, 1, local_segs - TAILS[mine] - 1, pair_recv.at[pair])
-        send(step + 1, rest_at, width, 0, local_segs - TAILS[1 - mine], pair_recv.at[pair])
+        send(step, rest_at, width - passed_columns, 0, 1, pair_recv.at[pair], held)
+        send(step, rest_at, width, 1, local_segs - TAILS[mine] - 1, pair_recv.at[pair], held)
+        send(step + 1, rest_at, width, 0, local_segs - TAILS[1 - mine], pair_recv.at[pair], held)
 
     def step_to(pair, target):
         return pair * PAIR + lax.rem(core + target, PAIR)
@@ -238,6 +240,23 @@
         def _():
             upward(group).wait_recv()
 
+    def send_first(held):
+        for step in range(3 * size, 3 * size + PAIR):
+            send_edge(step, held)
+        if passes:
+            for mine in range(PAIR):
+
+                @pl.when(jnp.logical_and(band == 1, core == mine))
+                def _():
+                    send_lead_passing(mine, held)
+
+            @pl.when(band == 0)
+            def _():
+                send_lead(3, held)
+
+        else:
+            send_lead(3, held)
+
     barrier = pltpu.get_barrier_semaphore()
 
     @pl.when(inner)
@@ -246,22 +265,23 @@
             greet(step, barrier)
         for step in range(size, 2 * size):
             greet(step, barrier)
+
+        @pl.when(plane == 1)
+        def _():
+            for step in range(PAIR):
+                rows_of = pl.ds(pl.multiple_of(partner(me, 3 * size + step, nseg) * rows, rows), rows)
+                pltpu.make_async_copy(coarse.at[:, rows_of, :], ahead.at[step], ahead_sem).start()
+
         pl.semaphore_wait(barrier, PAIR)
-        for step in range(3 * size, 3 * size + PAIR):
-            send_edge(step)
-        if passes:
-            for mine in range(PAIR):
-
-                @pl.when(jnp.logical_and(band == 1, core == mine))
-                def _():
-                    send_lead_passing(mine)
-
-            @pl.when(band == 0)
-            def _():
-                send_lead(3)
-
-        else:
-            send_lead(3)
+
+        @pl.when(plane == 1)
+        def _():
+            wait_for(ahead, ahead_sem)
+            send_first(ahead)
+
+        @pl.when(plane == 2)
+        def _():
+            send_first(None)
 
     @pl.when(outer)
     def _():
@@ -562,6 +582,7 @@
                 pltpu.VMEM((spins, CHUNK, EDGE), jnp.float32),
                 pltpu.VMEM((PAIR * max(parts), CHUNK + 2 * HALO, EDGE), jnp.float32),
                 pltpu.VMEM((1, rows, bins * PASSED // 8), jnp.float32),
+                pltpu.VMEM((PAIR, local_segs, rows, bins), jnp.float32),
                 pltpu.VMEM((nfreq, rows, EDGE), jnp.float32),
                 pltpu.SMEM(offsets.shape[::-1], jnp.int32),
                 dma,
@@ -580,6 +601,7 @@
                 signal,
                 dma,
                 dma,
+                dma,
             ],
             compiler_params=pltpu.CompilerParams(
                 collective_id=0, has_side_effects=True, vmem_limit_bytes=32 << 20

time: 53 us -> 53 us (level)
  no operation moved by 1% of the time
where the time goes in v2:
time: 53 us; the launch traced here: 52.6 us
  Pallas kernels  51.9 us (98%)
  between operations  0.64 us (1%)
    pallas_call x1, Pallas kernels, on_device(): pl.pallas_call(functools.partial(kernel, nseg, nfreq, parts), out_shape=j...  50.9 us

profile of v2, /device:TPU:8, one launch (start us, length us, event | category | flops | bytes accessed | tf_op | source)
XLA Modules:
  0.0 52.6 jit_solution(7555123674435588256)
XLA Ops:
  0.6 50.9 %shard_map.41.total = f32[33,8,1024]{2,1,0:T(8,128)S(1)} custom-call(f32[4,128,1024]{2,1,0:T(8,128)} %coarse.1, s32[32,64]{1,0:T(8,128)} %bitcast.1), custom_call_target="tpu_custom_call" | custom-call | tf_op jit(solution)/shard_map/pallas_call | solution.py:572
  51.6 1.0 %shard_map.42 = (f32[32,8,1024]{2,1,0:T(8,128)}, f32[8]{0:T(128)}) custom-call(f32[33,8,1024]{2,1,0:T(8,128)S(1)} %shard_map.41.total), custom_call_target="tpu_custom_call" | custom-call | tf_op jit(solution)/shard_map/pallas_call | solution.py:610
